TPU v7x, 32 devices: a whole 2x2x4 slice. The times are simulated.
32 devices in a mesh: leaf: 32 (over z, y, x, core).
Axes of the slice: x: 2, y: 2, z: 4, core: 2. Of those that a mesh axis runs over, the one named last changes fastest.
Arguments:
- panels: bfloat16 [64, 64, 256], P('leaf'), may hold values from -6 to 6
- basis: bfloat16 [64, 64, 256], P('leaf'), may hold values from -0.375 to 0.375
- transfer: bfloat16 [64, 64, 64], P('leaf'), may hold values from -0.25 to 0.25
- near_blocks: bfloat16 [64, 27, 256, 256], P('leaf'), may hold values from -0.078125 to 0.078125
- coupling: bfloat16 [2, 343, 4096], replicated, may hold values from -0.0546875 to 0.0546875
- near_list: int32 [64, 27], P('leaf'), may hold values from -1 to 63, as said below
Outputs:
- product: bfloat16 [64, 64, 256], P('leaf')
Inputs may be any that keep to these rules, and one draw needn't show every extreme that they name: `near_list`: row i lists, in an order of no meaning, leaf i and the leaves whose grid positions differ from it by at most one in each coordinate; -1 fills the other slots.
All inputs are finite; a program needn't handle non-finite values.
Results may differ from a plain program's by a relative error of at most 0.0035.
Values may be sent and summed in bfloat16 or wider, within the bound.
A program may use at most 192 MiB of HBM per device.

v0:
```python
import functools

import jax
import jax.numpy as jnp
from jax import lax
from jax.experimental import pallas as pl
from jax.experimental.pallas import tpu as pltpu
from jax.sharding import PartitionSpec as P

MESH = pl.DeviceIdType.MESH
F32 = jnp.float32
BF16 = jnp.bfloat16
REACH = 3
SPAN = 2 * REACH + 1
TN = (((0,), (0,)), ((), ()))
NT = (((1,), (1,)), ((), ()))
OFFSETS = [(a, b, c) for a in (-1, 0, 1) for b in (-1, 0, 1) for c in (-1, 0, 1)]


def axis_bits(first, bit_count):
    return [[b for b in range(bit_count) if (b + first) % 3 == a] for a in range(3)]


def coords_of(index, bits):
    return [
        sum(((index // 2**b) % 2) * 2**p for p, b in enumerate(bits[a])) + index * 0
        for a in range(3)
    ]


def index_of(coords, bits):
    return sum(((coords[a] // 2**p) % 2) * 2**b for a in range(3) for p, b in enumerate(bits[a]))


def inside(coords, bits):
    ok = None
    for a in range(3):
        here = (coords[a] >= 0) & (coords[a] < 2 ** len(bits[a]))
        ok = here if ok is None else ok & here
    return ok


def far_sum(targets, bit_count, stacked, table, pitch, rank):
    half = rank // 2
    bits = axis_bits(0, bit_count - 3)
    count = 2 ** (bit_count - 3)
    home = [c // 2 for c in targets[0]]
    everywhere = count <= 27

    def step(i, total):
        if everywhere:
            upper = coords_of(i, bits)
            q = i
            ok = None
            for a in range(3):
                near = jnp.abs(upper[a] - home[a]) <= 1
                ok = near if ok is None else ok & near
        else:
            upper = [home[0] + i // 9 - 1, home[1] + (i // 3) % 3 - 1, home[2] + i % 3 - 1]
            ok = inside(upper, bits)
            q = jnp.where(ok, index_of([jnp.maximum(u, 0) for u in upper], bits), 0)
        mats = []
        for target in targets:
            column = []
            for h in range(8):
                d = [2 * upper[a] + (h >> a & 1) - target[a] for a in range(3)]
                apart = (jnp.abs(d[0]) > 1) | (jnp.abs(d[1]) > 1) | (jnp.abs(d[2]) > 1)
                use = ok & apart
                code = (SPAN * (d[0] + REACH) + d[1] + REACH) * SPAN + d[2] + REACH
                code = jnp.where(use, code, 0)
                mat = table[pl.ds(code, half, stride=pitch), :]
                mat = mat * jnp.where(use, 1.0, 0.0).astype(F32)
                column.append(mat.astype(BF16))
            mats.append(jnp.concatenate(column, axis=0))
        mats = jnp.concatenate(mats, axis=1) if len(mats) > 1 else mats[0]
        rows = pl.ds(pl.multiple_of(q * 8 * half, 8 * half), 8 * half)
        return total + lax.dot_general(
            stacked[rows, :], mats, TN, preferred_element_type=F32
        )

    start = jnp.zeros((2 * rank, 2 * rank * len(targets)), F32)
    total = lax.fori_loop(0, min(count, 27), step, start)
    result = []
    for l in range(len(targets)):
        part = total[:, 2 * rank * l : 2 * rank * (l + 1)]
        result.append(part[:rank, :rank] + part[rank:, rank:])
    return result


def kernel(
    n,
    panels,
    basis,
    transfer,
    blocks_hbm,
    coupling_hbm,
    near_list,
    out,
    all_panels,
    blocks,
    coupling,
    table0,
    table1,
    coefs,
    parts,
    clusters,
    blocks_sem,
    coupling_sem,
    panel_send,
    panel_recv,
    coef_send,
    coef_recv,
    relay_send,
    relay_recv,
    part_send,
    part_recv,
    cluster_send,
    cluster_recv,
):
    leaf_dev, columns, points = panels.shape
    rank = basis.shape[1]
    slots = near_list.shape[1]
    half = rank // 2
    pitch = table0.shape[0] // half
    shifts = coupling.shape[1]
    low_bits = leaf_dev.bit_length() - 1
    dev_bits = n.bit_length() - 1
    bit_count = low_bits + dev_bits
    group = 8 // leaf_dev
    groups = n // group
    chips = n // 2
    own_rows = leaf_dev * half
    me = lax.axis_index("leaf")
    chip, core = me // 2, me % 2
    mate = chip * 2 + 1 - core

    loads = []
    for level in range(2):
        loads.append(
            pltpu.make_async_copy(
                coupling_hbm.at[level], coupling.at[level], coupling_sem.at[level]
            )
        )
    cut = slots // 3 if slots % 3 == 0 else slots
    for l in range(leaf_dev):
        for i in range(slots // cut):
            rows = pl.ds(i * cut, cut)
            loads.append(
                pltpu.make_async_copy(
                    blocks_hbm.at[l, rows],
                    blocks.at[l, rows],
                    blocks_sem.at[l * (slots // cut) + i],
                )
            )
    for load in loads:
        load.start()

    barrier = pltpu.get_barrier_semaphore()

    @pl.loop(1, n)
    def _(j):
        pl.semaphore_signal(
            barrier, inc=1, device_id=(lax.rem(me + j, n),), device_id_type=MESH
        )

    row = lax.broadcasted_iota(jnp.int32, (rank, rank), 0)
    col = lax.broadcasted_iota(jnp.int32, (rank, rank), 1)
    source = 2 * (row % half) + row // half
    order = jnp.where(col == source, 1.0, 0.0).astype(BF16)
    term = jnp.zeros((rank, columns), F32)
    for l in range(leaf_dev):
        flat = lax.dot_general(
            basis[l], panels[l], NT, preferred_element_type=F32
        ).astype(BF16)
        mixed = jnp.dot(order, flat, preferred_element_type=F32).astype(BF16)
        packed = jnp.concatenate([mixed[:half], mixed[half:]], axis=1)
        at = pl.multiple_of(me * own_rows, own_rows) + l * half
        coefs[pl.ds(pl.multiple_of(at, half), half), :] = packed
        sent = lax.dot_general(
            order, transfer[l], NT, preferred_element_type=F32
        ).astype(BF16)
        term = term + jnp.dot(sent, flat, preferred_element_type=F32)
    parts[0] = jnp.concatenate([term[:half], term[half:]], axis=1)
    for l in range(leaf_dev):
        all_panels[me * leaf_dev + l] = panels[l]

    pl.semaphore_wait(barrier, n - 1)

    def own_block(device):
        return coefs.at[pl.ds(pl.multiple_of(device * own_rows, own_rows), own_rows), :]

    def coef_copy(m, device):
        to = lax.rem(chip + m, chips) * 2 + core
        return pltpu.make_async_remote_copy(
            src_ref=own_block(device),
            dst_ref=own_block(device),
            send_sem=coef_send.at[m],
            recv_sem=coef_recv.at[m],
            device_id=(to,),
            device_id_type=MESH,
        )

    def relay_copy(m, device):
        return pltpu.make_async_remote_copy(
            src_ref=own_block(device),
            dst_ref=own_block(device),
            send_sem=relay_send.at[m],
            recv_sem=relay_recv.at[m],
            device_id=(mate,),
            device_id_type=MESH,
        )

    def part_copy(j):
        base = (me // group) * group
        return pltpu.make_async_remote_copy(
            src_ref=parts.at[0],
            dst_ref=parts.at[j],
            send_sem=part_send.at[j],
            recv_sem=part_recv.at[j],
            device_id=(base + lax.rem(me - base + j, group),),
            device_id_type=MESH,
        )

    def cluster_block(p):
        return clusters.at[pl.ds(pl.multiple_of(p * half, half), half), :]

    def cluster_copy(j, p):
        return pltpu.make_async_remote_copy(
            src_ref=cluster_block(p),
            dst_ref=cluster_block(p),
            send_sem=cluster_send.at[j],
            recv_sem=cluster_recv.at[j],
            device_id=(lax.rem(me + j * group, n),),
            device_id_type=MESH,
        )

    bits = axis_bits(low_bits, dev_bits)
    where = coords_of(me, bits)

    def panel_copy(o, sender, receiver):
        first, count = 0, leaf_dev
        if leaf_dev == 2 and OFFSETS[o][0] != 0:
            first, count = (1 if OFFSETS[o][0] > 0 else 0), 1
        return pltpu.make_async_remote_copy(
            src_ref=panels.at[pl.ds(first, count)],
            dst_ref=all_panels.at[pl.ds(sender * leaf_dev + first, count)],
            send_sem=panel_send.at[o],
            recv_sem=panel_recv.at[o],
            device_id=(receiver,),
            device_id_type=MESH,
        )

    def shifted(o, sign):
        moved = [where[a] + sign * OFFSETS[o][a] for a in range(3)]
        ok = inside(moved, bits)
        return ok, jnp.where(ok, index_of([jnp.maximum(v, 0) for v in moved], bits), 0)

    reach = [o for o in range(27) if OFFSETS[o] != (0, 0, 0)]

    for j in range(1, group):
        part_copy(j).start()
    relay_copy(0, me).start()

    @pl.loop(1, chips)
    def _(m):
        coef_copy(m, me).start()

    for o in reach:
        ok, to = shifted(o, 1)

        @pl.when(ok)
        def _():
            panel_copy(o, me, to).start()

    def unfold(level, table):
        @pl.loop(0, half)
        def _(k):
            lanes = pl.ds(pl.multiple_of(k * 2 * rank, 2 * rank), 2 * rank)
            rows = pl.ds(pl.multiple_of(k * pitch, 8), shifts)
            table[rows, :] = coupling[level, :, lanes].astype(F32)

    for j in range(1, group):
        part_copy(j).wait_recv()
    mine = me // group
    total = parts[0]
    for j in range(1, group):
        total = total + parts[j]
    clusters[pl.ds(pl.multiple_of(mine * half, half), half), :] = total.astype(BF16)
    loads[0].wait()
    unfold(0, table0)

    @pl.loop(1, groups)
    def _(j):
        cluster_copy(j, mine).start()

    @pl.loop(1, chips)
    def _(m):
        coef_copy(m, me).wait_recv()
        relay_copy(m, lax.rem(chip - m + chips, chips) * 2 + core).start()

    loads[1].wait()
    unfold(1, table1)

    @pl.loop(0, chips)
    def _(m):
        relay_copy(m, me).wait_recv()

    leaf_bits = axis_bits(0, bit_count)
    targets = [coords_of(me * leaf_dev + l, leaf_bits) for l in range(leaf_dev)]
    leaf_far = far_sum(targets, bit_count, coefs, table0, pitch, rank)

    @pl.loop(1, groups)
    def _(j):
        cluster_copy(j, mine).wait_recv()

    parent = coords_of(mine, axis_bits(0, bit_count - 3))
    down = far_sum([parent], bit_count - 3, clusters, table1, pitch, rank)[0].astype(BF16)
    far_terms = []
    for l in range(leaf_dev):
        far = leaf_far[l] + lax.dot_general(down, transfer[l], NT, preferred_element_type=F32)
        far_terms.append(jnp.dot(far.astype(BF16), basis[l], preferred_element_type=F32))

    for o in reach:
        ok, sender = shifted(o, -1)

        @pl.when(ok)
        def _():
            panel_copy(o, sender, me).wait_recv()

    for load in loads[2:]:
        load.wait()
    for l in range(leaf_dev):
        total = far_terms[l]
        for k in range(slots):
            j = near_list[l, k]
            block = all_panels[jnp.maximum(j, 0)]
            block = jnp.where(j >= 0, block, jnp.zeros_like(block))
            total = total + jnp.dot(block, blocks[l, k], preferred_element_type=F32)
        out[l] = total.astype(BF16)

    for j in range(1, group):
        part_copy(j).wait_send()

    @pl.loop(0, chips)
    def _(m):
        relay_copy(m, me).wait_send()

    @pl.loop(1, chips)
    def _(m):
        coef_copy(m, me).wait_send()

    @pl.loop(1, groups)
    def _(j):
        cluster_copy(j, mine).wait_send()

    for o in reach:
        ok, to = shifted(o, 1)

        @pl.when(ok)
        def _():
            panel_copy(o, me, to).wait_send()


def per_device(panels, basis, transfer, near_blocks, coupling, near_list):
    n = lax.axis_size("leaf")
    leaf_dev, columns, points = panels.shape
    rank = basis.shape[1]
    slots = near_list.shape[1]
    shifts = coupling.shape[1]
    half = rank // 2
    pitch = -(-shifts // 8) * 8
    leaves = n * leaf_dev
    group = 8 // leaf_dev
    vmem = pl.BlockSpec(memory_space=pltpu.VMEM)
    hbm = pl.BlockSpec(memory_space=pl.ANY)
    dma = pltpu.SemaphoreType.DMA
    return pl.pallas_call(
        functools.partial(kernel, n),
        out_shape=jax.ShapeDtypeStruct(panels.shape, BF16),
        in_specs=[vmem, vmem, vmem, hbm, hbm, pl.BlockSpec(memory_space=pltpu.SMEM)],
        out_specs=vmem,
        scratch_shapes=[
            pltpu.VMEM((leaves, columns, points), BF16),
            pltpu.VMEM(near_blocks.shape, BF16),
            pltpu.VMEM(coupling.shape, BF16),
            pltpu.VMEM((half * pitch, 2 * rank), F32),
            pltpu.VMEM((half * pitch, 2 * rank), F32),
            pltpu.VMEM((leaves * half, 2 * columns), BF16),
            pltpu.VMEM((group, half, 2 * columns), F32),
            pltpu.VMEM((n // group * half, 2 * columns), BF16),
            dma((leaf_dev * 3,)),
            dma((2,)),
            dma((27,)),
            dma((27,)),
            dma((n // 2,)),
            dma((n // 2,)),
            dma((n // 2,)),
            dma((n // 2,)),
            dma((group,)),
            dma((group,)),
            dma((n // group,)),
            dma((n // group,)),
        ],
        compiler_params=pltpu.CompilerParams(
            collective_id=0, has_side_effects=True, vmem_limit_bytes=60 * 2**20
        ),
    )(panels, basis, transfer, near_blocks, coupling, near_list)


def solution(mesh):
    placed = (
        P("leaf", None, None),
        P("leaf", None, None),
        P("leaf", None, None),
        P("leaf", None, None, None),
        P(),
        P("leaf", None),
    )
    return jax.shard_map(
        per_device, mesh=mesh, in_specs=placed, out_specs=P("leaf", None, None), check_vma=False
    )
```

profile of v0, /device:TPU:0, one launch (start us, length us, event | category | flops | bytes accessed | tf_op | source)
XLA Modules:
  0.0 40.7 jit_solution(11239318143769484835)
XLA Ops:
  0.0 9.0 %copy.7.coupling_hbm = bf16[2,343,4096]{2,1,0:T(8,128)(2,1)} copy(bf16[2,343,4096]{2,0,1:T(2,128)(2,1)} %param.10) | data formatting | bytes 11239424 | tf_op args[4]
  9.0 30.2 %shard_map.64 = bf16[2,64,256]{2,1,0:T(8,128)(2,1)} custom-call(bf16[2,64,256]{2,1,0:T(8,128)(2,1)} %panels.1, bf16[2,64,256]{2,1,0:T(8,128)(2,1)} %basis.1, bf16[2,64,64]{2,1,0:T(8,128)(2,1)} %transfer.1, bf16[2,27,256,256]{3,2,1,0:T(8,128)(2,1)} %blocks_hbm.1, bf16[2,343,4096]{2,1,0:T(8,128)(2,1)} %copy.7.coupling_hbm, s32[2,27]{1,0:T(2,128)} %near_list.1), custom_call_target="tpu_custom_call" | custom-call | tf_op jit(solution)/shard_map/pallas_call | solution.py:377
  39.2 1.5 %copy.9 = bf16[2,64,256]{2,1,0:T(8,128)(2,1)} copy(bf16[2,64,256]{2,1,0:T(8,128)(2,1)} %shard_map.64) | data formatting | bytes 131072
where the time goes:
time: 41.4 us; the launch traced here: 40.7 us
  Pallas kernels  30.2 us (73%)
  local copies, waits for them, and re-layouts  10.5 us (25%)
    pallas_call x1, Pallas kernels, per_device(): pl.pallas_call(functools.partial(kernel, n), out_shape=jax.ShapeDtypeStru...  30.2 us
    unnamed x2, local copies, waits for them, and re-layouts  10.5 us

commit v1 on v0

--- a/solution.py
+++ b/solution.py
@@ -40,27 +40,15 @@
     return ok
 
 
-def far_sum(targets, bit_count, stacked, table, pitch, rank):
-    half = rank // 2
-    bits = axis_bits(0, bit_count - 3)
+def far_mats(targets, bit_count, coupling, level, spread, mats):
+    half = coupling.shape[1] // 2
     count = 2 ** (bit_count - 3)
-    home = [c // 2 for c in targets[0]]
-    everywhere = count <= 27
-
-    def step(i, total):
-        if everywhere:
-            upper = coords_of(i, bits)
-            q = i
-            ok = None
-            for a in range(3):
-                near = jnp.abs(upper[a] - home[a]) <= 1
-                ok = near if ok is None else ok & near
-        else:
-            upper = [home[0] + i // 9 - 1, home[1] + (i // 3) % 3 - 1, home[2] + i % 3 - 1]
-            ok = inside(upper, bits)
-            q = jnp.where(ok, index_of([jnp.maximum(u, 0) for u in upper], bits), 0)
-        mats = []
-        for target in targets:
+
+    @pl.loop(0, min(count, 27))
+    def _(i):
+        upper, _, ok = candidate(targets[0], bit_count, i)
+        columns = []
+        for l, target in enumerate(targets):
             column = []
             for h in range(8):
                 d = [2 * upper[a] + (h >> a & 1) - target[a] for a in range(3)]
@@ -68,15 +56,38 @@
                 use = ok & apart
                 code = (SPAN * (d[0] + REACH) + d[1] + REACH) * SPAN + d[2] + REACH
                 code = jnp.where(use, code, 0)
-                mat = table[pl.ds(code, half, stride=pitch), :]
+                at = (l * 8 + h) * 2 * half
+                spread[at : at + 2 * half, :] = coupling[code].astype(F32)
+                mat = spread[pl.ds(at + level, half, stride=2), :]
                 mat = mat * jnp.where(use, 1.0, 0.0).astype(F32)
                 column.append(mat.astype(BF16))
-            mats.append(jnp.concatenate(column, axis=0))
-        mats = jnp.concatenate(mats, axis=1) if len(mats) > 1 else mats[0]
-        rows = pl.ds(pl.multiple_of(q * 8 * half, 8 * half), 8 * half)
-        return total + lax.dot_general(
-            stacked[rows, :], mats, TN, preferred_element_type=F32
-        )
+            columns.append(jnp.concatenate(column, axis=0))
+        mats[i] = jnp.concatenate(columns, axis=1) if len(columns) > 1 else columns[0]
+
+
+def candidate(target, bit_count, i):
+    bits = axis_bits(0, bit_count - 3)
+    home = [c // 2 for c in target]
+    if 2 ** (bit_count - 3) <= 27:
+        upper = coords_of(i, bits)
+        ok = None
+        for a in range(3):
+            near = jnp.abs(upper[a] - home[a]) <= 1
+            ok = near if ok is None else ok & near
+        return upper, i, ok
+    upper = [home[0] + i // 9 - 1, home[1] + (i // 3) % 3 - 1, home[2] + i % 3 - 1]
+    ok = inside(upper, bits)
+    return upper, jnp.where(ok, index_of([jnp.maximum(u, 0) for u in upper], bits), 0), ok
+
+
+def far_sum(targets, bit_count, stacked, mats, rank):
+    depth = 8 * rank // 2
+    count = 2 ** (bit_count - 3)
+
+    def step(i, total):
+        _, q, _ = candidate(targets[0], bit_count, i)
+        rows = pl.ds(pl.multiple_of(q * depth, depth), depth)
+        return total + lax.dot_general(stacked[rows, :], mats[i], TN, preferred_element_type=F32)
 
     start = jnp.zeros((2 * rank, 2 * rank * len(targets)), F32)
     total = lax.fori_loop(0, min(count, 27), step, start)
@@ -99,8 +110,9 @@
     all_panels,
     blocks,
     coupling,
-    table0,
-    table1,
+    spread,
+    mats0,
+    mats1,
     coefs,
     parts,
     clusters,
@@ -121,8 +133,6 @@
     rank = basis.shape[1]
     slots = near_list.shape[1]
     half = rank // 2
-    pitch = table0.shape[0] // half
-    shifts = coupling.shape[1]
     low_bits = leaf_dev.bit_length() - 1
     dev_bits = n.bit_length() - 1
     bit_count = low_bits + dev_bits
@@ -134,13 +144,7 @@
     chip, core = me // 2, me % 2
     mate = chip * 2 + 1 - core
 
-    loads = []
-    for level in range(2):
-        loads.append(
-            pltpu.make_async_copy(
-                coupling_hbm.at[level], coupling.at[level], coupling_sem.at[level]
-            )
-        )
+    loads = [pltpu.make_async_copy(coupling_hbm, coupling, coupling_sem)]
     cut = slots // 3 if slots % 3 == 0 else slots
     for l in range(leaf_dev):
         for i in range(slots // cut):
@@ -272,13 +276,6 @@
         def _():
             panel_copy(o, me, to).start()
 
-    def unfold(level, table):
-        @pl.loop(0, half)
-        def _(k):
-            lanes = pl.ds(pl.multiple_of(k * 2 * rank, 2 * rank), 2 * rank)
-            rows = pl.ds(pl.multiple_of(k * pitch, 8), shifts)
-            table[rows, :] = coupling[level, :, lanes].astype(F32)
-
     for j in range(1, group):
         part_copy(j).wait_recv()
     mine = me // group
@@ -286,8 +283,9 @@
     for j in range(1, group):
         total = total + parts[j]
     clusters[pl.ds(pl.multiple_of(mine * half, half), half), :] = total.astype(BF16)
+    parent = coords_of(mine, axis_bits(0, bit_count - 3))
     loads[0].wait()
-    unfold(0, table0)
+    far_mats([parent], bit_count - 3, coupling, 1, spread, mats1)
 
     @pl.loop(1, groups)
     def _(j):
@@ -298,23 +296,21 @@
         coef_copy(m, me).wait_recv()
         relay_copy(m, lax.rem(chip - m + chips, chips) * 2 + core).start()
 
-    loads[1].wait()
-    unfold(1, table1)
+    leaf_bits = axis_bits(0, bit_count)
+    targets = [coords_of(me * leaf_dev + l, leaf_bits) for l in range(leaf_dev)]
+    far_mats(targets, bit_count, coupling, 0, spread, mats0)
 
     @pl.loop(0, chips)
     def _(m):
         relay_copy(m, me).wait_recv()
 
-    leaf_bits = axis_bits(0, bit_count)
-    targets = [coords_of(me * leaf_dev + l, leaf_bits) for l in range(leaf_dev)]
-    leaf_far = far_sum(targets, bit_count, coefs, table0, pitch, rank)
+    leaf_far = far_sum(targets, bit_count, coefs, mats0, rank)
 
     @pl.loop(1, groups)
     def _(j):
         cluster_copy(j, mine).wait_recv()
 
-    parent = coords_of(mine, axis_bits(0, bit_count - 3))
-    down = far_sum([parent], bit_count - 3, clusters, table1, pitch, rank)[0].astype(BF16)
+    down = far_sum([parent], bit_count - 3, clusters, mats1, rank)[0].astype(BF16)
     far_terms = []
     for l in range(leaf_dev):
         far = leaf_far[l] + lax.dot_general(down, transfer[l], NT, preferred_element_type=F32)
@@ -327,7 +323,7 @@
         def _():
             panel_copy(o, sender, me).wait_recv()
 
-    for load in loads[2:]:
+    for load in loads[1:]:
         load.wait()
     for l in range(leaf_dev):
         total = far_terms[l]
@@ -368,8 +364,9 @@
     slots = near_list.shape[1]
     shifts = coupling.shape[1]
     half = rank // 2
-    pitch = -(-shifts // 8) * 8
     leaves = n * leaf_dev
+    coupling = coupling.transpose(1, 0, 2).reshape(shifts, 2, half, 2 * rank)
+    coupling = coupling.transpose(0, 2, 1, 3).reshape(shifts, rank, 2 * rank)
     group = 8 // leaf_dev
     vmem = pl.BlockSpec(memory_space=pltpu.VMEM)
     hbm = pl.BlockSpec(memory_space=pl.ANY)
@@ -383,13 +380,14 @@
             pltpu.VMEM((leaves, columns, points), BF16),
             pltpu.VMEM(near_blocks.shape, BF16),
             pltpu.VMEM(coupling.shape, BF16),
-            pltpu.VMEM((half * pitch, 2 * rank), F32),
-            pltpu.VMEM((half * pitch, 2 * rank), F32),
+            pltpu.VMEM((leaf_dev * 8 * rank, 2 * rank), F32),
+            pltpu.VMEM((min(leaves // 8, 27), 8 * half, 2 * rank * leaf_dev), BF16),
+            pltpu.VMEM((min(leaves // 64, 27), 8 * half, 2 * rank), BF16),
             pltpu.VMEM((leaves * half, 2 * columns), BF16),
             pltpu.VMEM((group, half, 2 * columns), F32),
             pltpu.VMEM((n // group * half, 2 * columns), BF16),
             dma((leaf_dev * 3,)),
-            dma((2,)),
+            dma,
             dma((27,)),
             dma((27,)),
             dma((n // 2,)),

time: 41.4 us -> 32.3 us (0.78)
  the two profiles are of different devices: /device:TPU:0 before, /device:TPU:1 now
where the time goes in v1:
time: 32.3 us; the launch traced here: 32.1 us
  Pallas kernels  30.6 us (95%)
  local copies, waits for them, and re-layouts  1.47 us (5%)
    pallas_call x1, Pallas kernels, per_device(): pl.pallas_call(functools.partial(kernel, n), out_shape=jax.ShapeDtypeStru...  30.6 us
    unnamed x1, local copies, waits for them, and re-layouts  1.47 us

profile of v1, /device:TPU:1, one launch (start us, length us, event | category | flops | bytes accessed | tf_op | source)
XLA Modules:
  0.0 32.1 jit_solution(531853739422617129)
XLA Ops:
  0.0 30.6 %shard_map.64 = bf16[2,64,256]{2,1,0:T(8,128)(2,1)} custom-call(bf16[2,64,256]{2,1,0:T(8,128)(2,1)} %panels.1, bf16[2,64,256]{2,1,0:T(8,128)(2,1)} %basis.1, bf16[2,64,64]{2,1,0:T(8,128)(2,1)} %transfer.1, bf16[2,27,256,256]{3,2,1,0:T(8,128)(2,1)} %blocks_hbm.1, bf16[343,64,128]{2,1,0:T(8,128)(2,1)} %bitcast.7, s32[2,27]{1,0:T(2,128)} %near_list.1), custom_call_target="tpu_custom_call" | custom-call | tf_op jit(solution)/shard_map/pallas_call | solution.py:374
  30.6 1.5 %copy.9 = bf16[2,64,256]{2,1,0:T(8,128)(2,1)} copy(bf16[2,64,256]{2,1,0:T(8,128)(2,1)} %shard_map.64) | data formatting | bytes 131072

commit v2 on v1

--- a/solution.py
+++ b/solution.py
@@ -193,14 +193,26 @@
     def own_block(device):
         return coefs.at[pl.ds(pl.multiple_of(device * own_rows, own_rows), own_rows), :]
 
-    def coef_copy(m, device):
-        to = lax.rem(chip + m, chips) * 2 + core
+    places = min(4, chips)
+    columns_of_chips = chips // places
+    line, place = chip // places, lax.rem(chip, places)
+
+    def coef_device(j, k):
+        from_line = lax.rem(line - j + columns_of_chips, columns_of_chips)
+        from_place = lax.rem(place - k + places, places)
+        return (from_line * places + from_place) * 2 + core
+
+    def coef_copy(j, k):
+        to_line = lax.rem(line + j, columns_of_chips) if k is None else line
+        to_place = place if k is None else lax.rem(place + k, places)
+        m = j * places + (0 if k is None else k)
+        block = own_block(me) if k is None else own_block(coef_device(j, 0))
         return pltpu.make_async_remote_copy(
-            src_ref=own_block(device),
-            dst_ref=own_block(device),
+            src_ref=block,
+            dst_ref=block,
             send_sem=coef_send.at[m],
             recv_sem=coef_recv.at[m],
-            device_id=(to,),
+            device_id=((to_line * places + to_place) * 2 + core,),
             device_id_type=MESH,
         )
 
@@ -241,40 +253,69 @@
     bits = axis_bits(low_bits, dev_bits)
     where = coords_of(me, bits)
 
-    def panel_copy(o, sender, receiver):
+    def hop_of(o):
+        x, y, z = OFFSETS[o]
+        return (0, y, 0) if y else (x, 0, 0) if x else (0, 0, z)
+
+    def moved(offset):
+        there = [where[a] + offset[a] for a in range(3)]
+        ok = inside(there, bits)
+        return ok, jnp.where(ok, index_of([jnp.maximum(v, 0) for v in there], bits), 0)
+
+    def panel_copy(o, source, receiver):
         first, count = 0, leaf_dev
         if leaf_dev == 2 and OFFSETS[o][0] != 0:
             first, count = (1 if OFFSETS[o][0] > 0 else 0), 1
+        rows = pl.ds(source * leaf_dev + first, count)
+        owned = hop_of(o) == OFFSETS[o]
         return pltpu.make_async_remote_copy(
-            src_ref=panels.at[pl.ds(first, count)],
-            dst_ref=all_panels.at[pl.ds(sender * leaf_dev + first, count)],
+            src_ref=panels.at[pl.ds(first, count)] if owned else all_panels.at[rows],
+            dst_ref=all_panels.at[rows],
             send_sem=panel_send.at[o],
             recv_sem=panel_recv.at[o],
             device_id=(receiver,),
             device_id_type=MESH,
         )
 
-    def shifted(o, sign):
-        moved = [where[a] + sign * OFFSETS[o][a] for a in range(3)]
-        ok = inside(moved, bits)
-        return ok, jnp.where(ok, index_of([jnp.maximum(v, 0) for v in moved], bits), 0)
+    def sends(o, act):
+        hop = hop_of(o)
+        ok, to = moved(hop)
+        known, source = moved([h - e for h, e in zip(hop, OFFSETS[o])])
+
+        @pl.when(ok & known)
+        def _():
+            act(panel_copy(o, source, to))
+
+    def receives(o):
+        known, source = moved([-e for e in OFFSETS[o]])
+
+        @pl.when(known)
+        def _():
+            panel_copy(o, source, me).wait_recv()
 
     reach = [o for o in range(27) if OFFSETS[o] != (0, 0, 0)]
+    along_z = [o for o in reach if not OFFSETS[o][0] and not OFFSETS[o][1]]
+    along_x = [o for o in reach if OFFSETS[o][0] and not OFFSETS[o][1]]
+    along_y = [o for o in reach if OFFSETS[o][1]]
+
+    def start(copy):
+        copy.start()
 
     for j in range(1, group):
         part_copy(j).start()
+    for o in along_z:
+        sends(o, start)
+
+    @pl.loop(1, columns_of_chips)
+    def _(j):
+        coef_copy(j, None).start()
+
     relay_copy(0, me).start()
-
-    @pl.loop(1, chips)
-    def _(m):
-        coef_copy(m, me).start()
-
-    for o in reach:
-        ok, to = shifted(o, 1)
-
-        @pl.when(ok)
-        def _():
-            panel_copy(o, me, to).start()
+    for k in range(1, places):
+        coef_copy(0, k).start()
+    for o in along_x + along_y:
+        if hop_of(o) == OFFSETS[o]:
+            sends(o, start)
 
     for j in range(1, group):
         part_copy(j).wait_recv()
@@ -283,21 +324,43 @@
     for j in range(1, group):
         total = total + parts[j]
     clusters[pl.ds(pl.multiple_of(mine * half, half), half), :] = total.astype(BF16)
+
+    for o in along_z:
+        receives(o)
+        for later in along_x + along_y:
+            before = [e - h for e, h in zip(OFFSETS[later], hop_of(later))]
+            if tuple(before) == OFFSETS[o]:
+                sends(later, start)
+
+    @pl.loop(1, columns_of_chips)
+    def _(j):
+        coef_copy(j, None).wait_recv()
+        for k in range(1, places):
+            coef_copy(j, k).start()
+        relay_copy(j * places, coef_device(j, 0)).start()
+
+    @pl.loop(1, groups)
+    def _(j):
+        cluster_copy(j, mine).start()
+
+    for o in along_x:
+        receives(o)
+        for later in along_y:
+            before = [e - h for e, h in zip(OFFSETS[later], hop_of(later))]
+            if tuple(before) == OFFSETS[o]:
+                sends(later, start)
+
+    @pl.loop(0, columns_of_chips)
+    def _(j):
+        for k in range(1, places):
+            coef_copy(j, k).wait_recv()
+            relay_copy(j * places + k, coef_device(j, k)).start()
+
     parent = coords_of(mine, axis_bits(0, bit_count - 3))
+    leaf_bits = axis_bits(0, bit_count)
+    targets = [coords_of(me * leaf_dev + l, leaf_bits) for l in range(leaf_dev)]
     loads[0].wait()
     far_mats([parent], bit_count - 3, coupling, 1, spread, mats1)
-
-    @pl.loop(1, groups)
-    def _(j):
-        cluster_copy(j, mine).start()
-
-    @pl.loop(1, chips)
-    def _(m):
-        coef_copy(m, me).wait_recv()
-        relay_copy(m, lax.rem(chip - m + chips, chips) * 2 + core).start()
-
-    leaf_bits = axis_bits(0, bit_count)
-    targets = [coords_of(me * leaf_dev + l, leaf_bits) for l in range(leaf_dev)]
     far_mats(targets, bit_count, coupling, 0, spread, mats0)
 
     @pl.loop(0, chips)
@@ -316,13 +379,8 @@
         far = leaf_far[l] + lax.dot_general(down, transfer[l], NT, preferred_element_type=F32)
         far_terms.append(jnp.dot(far.astype(BF16), basis[l], preferred_element_type=F32))
 
-    for o in reach:
-        ok, sender = shifted(o, -1)
-
-        @pl.when(ok)
-        def _():
-            panel_copy(o, sender, me).wait_recv()
-
+    for o in along_y:
+        receives(o)
     for load in loads[1:]:
         load.wait()
     for l in range(leaf_dev):
@@ -341,20 +399,21 @@
     def _(m):
         relay_copy(m, me).wait_send()
 
-    @pl.loop(1, chips)
-    def _(m):
-        coef_copy(m, me).wait_send()
+    @pl.loop(1, columns_of_chips)
+    def _(j):
+        coef_copy(j, None).wait_send()
+
+    @pl.loop(0, columns_of_chips)
+    def _(j):
+        for k in range(1, places):
+            coef_copy(j, k).wait_send()
 
     @pl.loop(1, groups)
     def _(j):
         cluster_copy(j, mine).wait_send()
 
     for o in reach:
-        ok, to = shifted(o, 1)
-
-        @pl.when(ok)
-        def _():
-            panel_copy(o, me, to).wait_send()
+        sends(o, lambda copy: copy.wait_send())
 
 
 def per_device(panels, basis, transfer, near_blocks, coupling, near_list):

time: 32.3 us -> 26.1 us (0.81)
  the two profiles are of different devices: /device:TPU:1 before, /device:TPU:0 now
where the time goes in v2:
time: 26.1 us; the launch traced here: 25.9 us
  Pallas kernels  24.4 us (93%)
  local copies, waits for them, and re-layouts  1.47 us (6%)
    pallas_call x1, Pallas kernels, per_device(): pl.pallas_call(functools.partial(kernel, n), out_shape=jax.ShapeDtypeStru...  24.4 us
    unnamed x1, local copies, waits for them, and re-layouts  1.47 us

profile of v2, /device:TPU:0, one launch (start us, length us, event | category | flops | bytes accessed | tf_op | source)
XLA Modules:
  0.0 25.9 jit_solution(8975640583852854730)
XLA Ops:
  0.0 24.4 %shard_map.64 = bf16[2,64,256]{2,1,0:T(8,128)(2,1)} custom-call(bf16[2,64,256]{2,1,0:T(8,128)(2,1)} %panels.1, bf16[2,64,256]{2,1,0:T(8,128)(2,1)} %basis.1, bf16[2,64,64]{2,1,0:T(8,128)(2,1)} %transfer.1, bf16[2,27,256,256]{3,2,1,0:T(8,128)(2,1)} %blocks_hbm.1, bf16[343,64,128]{2,1,0:T(8,128)(2,1)} %bitcast.7, s32[2,27]{1,0:T(2,128)} %near_list.1), custom_call_target="tpu_custom_call" | custom-call | tf_op jit(solution)/shard_map/pallas_call | solution.py:433
  24.4 1.5 %copy.9 = bf16[2,64,256]{2,1,0:T(8,128)(2,1)} copy(bf16[2,64,256]{2,1,0:T(8,128)(2,1)} %shard_map.64) | data formatting | bytes 131072

commit v3 on v2

--- a/solution.py
+++ b/solution.py
@@ -306,6 +306,10 @@
     for o in along_z:
         sends(o, start)
 
+    for o in along_x + along_y:
+        if hop_of(o) == OFFSETS[o]:
+            sends(o, start)
+
     @pl.loop(1, columns_of_chips)
     def _(j):
         coef_copy(j, None).start()
@@ -313,10 +317,6 @@
     relay_copy(0, me).start()
     for k in range(1, places):
         coef_copy(0, k).start()
-    for o in along_x + along_y:
-        if hop_of(o) == OFFSETS[o]:
-            sends(o, start)
-
     for j in range(1, group):
         part_copy(j).wait_recv()
     mine = me // group

time: 26.1 us -> 26.1 us (level)
  no operation moved by 1% of the time
where the time goes in v3:
time: 26.1 us; the launch traced here: 25.9 us
  Pallas kernels  24.4 us (93%)
  local copies, waits for them, and re-layouts  1.47 us (6%)
    pallas_call x1, Pallas kernels, per_device(): pl.pallas_call(functools.partial(kernel, n), out_shape=jax.ShapeDtypeStru...  24.4 us
    unnamed x1, local copies, waits for them, and re-layouts  1.47 us

profile of v3, /device:TPU:0, one launch (start us, length us, event | category | flops | bytes accessed | tf_op | source)
XLA Modules:
  0.0 25.9 jit_solution(14655175824824727873)
XLA Ops:
  0.0 24.4 %shard_map.64 = bf16[2,64,256]{2,1,0:T(8,128)(2,1)} custom-call(bf16[2,64,256]{2,1,0:T(8,128)(2,1)} %panels.1, bf16[2,64,256]{2,1,0:T(8,128)(2,1)} %basis.1, bf16[2,64,64]{2,1,0:T(8,128)(2,1)} %transfer.1, bf16[2,27,256,256]{3,2,1,0:T(8,128)(2,1)} %blocks_hbm.1, bf16[343,64,128]{2,1,0:T(8,128)(2,1)} %bitcast.7, s32[2,27]{1,0:T(2,128)} %near_list.1), custom_call_target="tpu_custom_call" | custom-call | tf_op jit(solution)/shard_map/pallas_call | solution.py:433
  24.4 1.5 %copy.9 = bf16[2,64,256]{2,1,0:T(8,128)(2,1)} copy(bf16[2,64,256]{2,1,0:T(8,128)(2,1)} %shard_map.64) | data formatting | bytes 131072
